TPU v7x, 256 devices: a whole 4x4x8 slice. The times are simulated.
256 devices in a mesh: group: 64 (over z, y_hi, x), replica: 4 (over y_lo, core).
Axes of the slice: x: 4, y: 4 (y_hi: 2, y_lo: 2; y = y_hi * 2 + y_lo), z: 8, core: 2. Of those that a mesh axis runs over, the one named last changes fastest.
Arguments:
- grad: bfloat16 [32768, 8192], P('group', 'replica'), may hold values from -45 to 45, as said below
- prev_left: bfloat16 [64, 512, 512], P('group', 'replica'), may hold values from -1 to 1.5
- prev_right: bfloat16 [16, 512, 512], P('replica', 'group'), may hold values from -1 to 1.5
- exp_left: int32 [64], P('group'), may hold values from -2 to 2
- exp_right: int32 [16], P('replica'), may hold values from -2 to 2
- strip_owner: int32 [64], replicated, may hold values from 0 to 63, each once
Outputs:
- precond: bfloat16 [32768, 8192], P('group', 'replica')
- root_left: bfloat16 [64, 512, 512], P('group', 'replica')
- root_right: bfloat16 [16, 64, 8, 512], P('replica', 'group')
Inputs may be any that keep to these rules, and one draw needn't show every extreme that they name: `grad`: entries have row and column scales of different sizes. `strip_owner`: each of 0 to 63 appears once.
All inputs are finite; a program needn't handle non-finite values.
Results may differ from a plain program's by a relative error of at most 0.0083.
Values may be sent and summed in bfloat16 or wider, within the bound.
A program may use at most 64 MiB of HBM per device.

v0:
```python
import jax
import jax.numpy as jnp
from jax import lax
from jax.sharding import Mesh
from jax.sharding import PartitionSpec as P

GROUP = ("group_0", "group_1", "group_2")
REPLICA = ("replica_0", "replica_1")
GROUP_REPLICA = ("group_0", "group_1", "group_2", "replica_0", "replica_1")
EPSILON = 1e-06


def over_axes(x, axes):
    for axis in axes:
        x = lax.psum(x, axis)
    return x


def cut_along(x, dim, devices):
    dims = x.shape
    pieces = x.reshape(*dims[:dim], devices, dims[dim] // devices, *dims[dim + 1 :])
    return jnp.moveaxis(pieces, dim, 0)


def sent_and_summed(x, axis, dim):
    pieces = cut_along(x, dim, lax.axis_size(axis))
    arrived = lax.all_to_all(pieces, axis, split_axis=0, concat_axis=0, tiled=True)
    return arrived.astype(jnp.float32).sum(axis=0)


def from_everyone(x, axis):
    copies = jnp.broadcast_to(x, (lax.axis_size(axis), *x.shape))
    return lax.all_to_all(copies, axis, split_axis=0, concat_axis=0, tiled=True)


def in_order(pieces, dim):
    pieces = jnp.moveaxis(pieces, 0, dim)
    dims = pieces.shape
    return pieces.reshape(*dims[:dim], dims[dim] * dims[dim + 1], *dims[dim + 2 :])


def collect(x, axis, dim):
    pieces = from_everyone(x, axis)
    return in_order(pieces, dim)


def pow_two(exponent):
    result = jnp.zeros(exponent.shape, jnp.float32)
    for power in range(-4, 5):
        result = result + jnp.where(exponent == power, jnp.float32(2.0**power), jnp.float32(0.0))
    return result


def newton_rows(gram_rows, gram_scale, start_root, start_rows):
    product = gram_rows / gram_scale
    for repeat in range(5):
        product = jnp.matmul(product, start_root, precision=lax.Precision.HIGHEST)
    return (5.0 * start_rows - product) / 4.0


def shards(grad, prev_left, prev_right, exp_left, exp_right, strip_owner):
    block_size = grad.shape[0]
    col_count = prev_right.shape[0]
    pieces = grad.reshape(block_size, col_count, block_size)
    groups = lax.axis_size(GROUP)
    replicas = lax.axis_size(REPLICA)
    group_index = lax.axis_index(GROUP)
    replica_index = lax.axis_index(REPLICA)
    strip_rows = block_size // groups
    square = jnp.sum(jnp.square(pieces.astype(jnp.float32)), axis=(0, 2))
    group_pick = (jnp.arange(groups) == group_index).astype(jnp.float32)
    replica_pick = (jnp.arange(replicas) == replica_index).astype(jnp.float32)
    norm_grid = group_pick[:, None, None] * replica_pick[None, :, None] * square[None, None, :]
    norm_grid = over_axes(norm_grid, GROUP_REPLICA)
    left_scale = jnp.sum(norm_grid * group_pick[:, None, None]) / block_size + EPSILON
    right_scale = (
        jnp.sum(norm_grid * replica_pick[None, :, None], axis=(0, 1)) / block_size + EPSILON
    )
    left_part = lax.dot_general(
        grad, grad, (((1,), (1,)), ((), ())), preferred_element_type=jnp.float32
    )
    right_part = lax.dot_general(
        pieces, pieces, (((0,), (0,)), ((1,), (1,))), preferred_element_type=jnp.float32
    )
    left_strip = sent_and_summed(left_part.astype(jnp.bfloat16), REPLICA, 0)
    owned_strip = strip_owner[group_index]
    reordered = right_part.reshape(col_count, groups, strip_rows, block_size)[:, strip_owner]
    reordered = reordered.reshape(col_count, block_size, block_size)
    right_strip = sent_and_summed(reordered.astype(jnp.bfloat16), GROUP, 1)
    left_start = collect(prev_left[0], REPLICA, 0).astype(jnp.float32)
    right_start = lax.all_gather(prev_right, GROUP, axis=1, tiled=True).astype(jnp.float32)
    left_rows = prev_left[0].astype(jnp.float32)
    right_rows = lax.dynamic_slice_in_dim(right_start, owned_strip * strip_rows, strip_rows, 1)
    left_new = newton_rows(left_strip, left_scale, left_start, left_rows)
    right_new = newton_rows(right_strip, right_scale[:, None, None], right_start, right_rows)
    left_code = (left_new * pow_two(-exp_left[0])).astype(jnp.bfloat16)
    right_code = (right_new * pow_two(-exp_right)[:, None, None]).astype(jnp.bfloat16)
    left_full = collect(left_code, REPLICA, 0)
    right_owned = lax.all_gather(right_code, GROUP, axis=1, tiled=True).reshape(
        col_count, groups, strip_rows, block_size
    )
    owner_match = strip_owner[:, None] == jnp.arange(groups)[None, :]
    inverse = jnp.sum(jnp.where(owner_match, jnp.arange(groups)[:, None], 0), axis=0)
    right_full = right_owned[:, inverse].reshape(col_count, block_size, block_size)
    left_dec = (left_full.astype(jnp.float32) * pow_two(exp_left[0])).astype(jnp.bfloat16)
    right_dec = (right_full.astype(jnp.float32) * pow_two(exp_right)[:, None, None]).astype(
        jnp.bfloat16
    )
    middle = lax.dot_general(
        pieces, right_dec, (((2,), (1,)), ((1,), (0,))), preferred_element_type=jnp.float32
    ).astype(jnp.bfloat16)
    result = lax.dot_general(
        left_dec, middle, (((1,), (1,)), ((), ())), preferred_element_type=jnp.float32
    ).astype(jnp.bfloat16)
    return (
        result.reshape(block_size, col_count * block_size),
        left_code[None],
        right_code[:, None],
    )


def solution(mesh):
    torus = Mesh(
        mesh.devices.reshape(8, 2, 4, 2, 2),
        ("group_0", "group_1", "group_2", "replica_0", "replica_1"),
    )
    in_specs = (
        P(GROUP, REPLICA),
        P(GROUP, REPLICA, None),
        P(REPLICA, GROUP, None),
        P(GROUP),
        P(REPLICA),
        P(),
    )
    out_specs = (P(GROUP, REPLICA), P(GROUP, REPLICA, None), P(REPLICA, GROUP, None, None))
    return jax.shard_map(
        shards, mesh=torus, in_specs=in_specs, out_specs=out_specs, check_vma=False
    )
```

profile of v0, /device:TPU:2, one launch (start us, length us, event | category | flops | bytes accessed | tf_op | source)
XLA Modules:
  0.0 278.3 jit_solution(7575325970475510265)
XLA Ops:
  7.2 3.5 %convolution_bitcast_fusion = bf16[4,64,8,512]{3,2,1,0:T(8,128)(2,1)S(1)} fusion(bf16[64,4,8,512]{3,2,1,0:T(8,128)(2,1)} %bitcast.77), kind=kOutput, calls=%fused_computation.7 | convolution fusion | flops 1073741824 | bytes 4194304 | tf_op jit(solution)/shard_map/dot_general | solution.py:82
  10.8 2.0 gather_fusion
  12.8 14.6 %all-to-all-start.3 = ((bf16[64,4,8,512]{3,2,1,0:T(8,128)(2,1)}), bf16[64,4,8,512]{3,2,1,0:T(8,128)(2,1)S(1)}, u32[]{:S(2)}, u32[]{:S(2)}) async-start(bf16[64,4,8,512]{3,2,1,0:T(8,128)(2,1)} %gather_fusion), calls=%async_computation.3 | async-start | bytes 4194304 | tf_op jit(solution)/shard_map/all_to_all | solution.py:27
  27.4 0.0 copy-start.4
  27.4 0.0 all-gather.3.cloned.1.call-start
  27.5 0.7 all-gather.3.cloned.1.call-update
  28.2 0.0 all-gather.5.cloned.1.call-start
  28.2 0.6 dynamic_slice.6
  29.5 2.0 multiply_reduce_fusion
  31.5 0.1 reduce_sum.66
  31.7 0.1 broadcast_multiply_fusion.1
  31.7 0.1 broadcast_multiply_fusion
  31.8 53.5 %psum.35 = f32[64,4,4]{0,2,1:T(4,128)S(1)} all-reduce(f32[64,4,4]{0,2,1:T(4,128)S(1)} %broadcast_multiply_fusion), channel_id=1, replica_groups=mesh['group_0'=8,'group_1'=2,'group_2'=4,'replica_0'=2,'replica_1'=2] {'..., use_global_device_ids=true, to_apply=%region_3.0 | all-reduce | flops 1024 | bytes 8192 | tf_op jit(solution)/shard_map/psum | solution.py:15
  85.3 6.5 %psum.36 = f32[64,4,4]{0,2,1:T(4,128)S(1)} all-reduce(f32[64,4,4]{0,2,1:T(4,128)S(1)} %psum.35), channel_id=1, replica_groups=mesh['group_0'=8,'group_1'=2,'group_2'=4,'replica_0'=2,'replica_1'=2] {'..., use_global_device_ids=true, to_apply=%region_4.0 | all-reduce | flops 1024 | bytes 8192 | tf_op jit(solution)/shard_map/psum | solution.py:15
  91.8 8.7 %psum.37 = f32[64,4,4]{0,2,1:T(4,128)S(1)} all-reduce(f32[64,4,4]{0,2,1:T(4,128)S(1)} %psum.36), channel_id=1, replica_groups=mesh['group_0'=8,'group_1'=2,'group_2'=4,'replica_0'=2,'replica_1'=2] {'..., use_global_device_ids=true, to_apply=%region_5.0 | all-reduce | flops 1024 | bytes 8192 | tf_op jit(solution)/shard_map/psum | solution.py:15
  100.5 5.0 %psum.38 = f32[64,4,4]{0,2,1:T(4,128)S(1)} all-reduce(f32[64,4,4]{0,2,1:T(4,128)S(1)} %psum.37), channel_id=1, replica_groups=mesh['group_0'=8,'group_1'=2,'group_2'=4,'replica_0'=2,'replica_1'=2] {'..., use_global_device_ids=true, to_apply=%region_6.0 | all-reduce | flops 1024 | bytes 8192 | tf_op jit(solution)/shard_map/psum | solution.py:15
  105.5 2.5 psum.39
  108.0 0.6 multiply_reduce_fusion.1
  108.7 0.3 convert_reduce_fusion
  109.0 36.6 %all-gather.3.cloned.1.call-done = bf16[4,512,512]{2,1,0:T(8,128)(2,1)} async-done(((bf16[4,8,512]{2,1,0:T(8,128)(2,1)}), bf16[4,512,512]{2,1,0:T(8,128)(2,1)}) %all-gather.3.cloned.1.call-update) | async-done | bytes 2097168 | tf_op jit(solution)/shard_map/all_gather | solution.py:91
  145.6 2.7 fusion.29
  148.3 0.9 fusion.53
  149.2 0.9 fusion.54
  150.1 0.9 fusion.55
  151.1 1.6 fusion.25
  152.6 0.0 all-gather.5.cloned.1.call-update
  152.7 0.0 copy-start.2
  152.7 1.3 convolution_convert_fusion
  153.9 11.3 %all_to_all.20 = bf16[4,128,512]{2,1,0:T(8,128)(2,1)S(1)} all-to-all(bf16[4,128,512]{2,1,0:T(8,128)(2,1)S(1)} %bitcast.81), channel_id=1, replica_groups=mesh['group_0'=8,'group_1'=2,'group_2'=4,'replica_0'=2,'replica_1'=2] {'..., dimensions={0} | all-to-all | bytes 1048576 | tf_op jit(solution)/shard_map/all_to_all | solution.py:27
  165.3 0.8 broadcast_in_dim.97
  166.1 3.5 %all-to-all-start.1 = ((bf16[4,128,512]{2,1,0:T(8,128)(2,1)}), bf16[4,128,512]{2,1,0:T(8,128)(2,1)S(1)}, u32[]{:S(2)}, u32[]{:S(2)}) async-start(bf16[4,128,512]{2,1,0:T(8,128)(2,1)} %broadcast_in_dim.97), calls=%async_computation.1 | async-start | bytes 1048576 | tf_op jit(solution)/shard_map/all_to_all | solution.py:33
  171.0 0.1 convert_reduce_fusion.1
  171.1 7.3 %all-to-all-done.1 = bf16[4,128,512]{2,1,0:T(8,128)(2,1)S(1)} async-done(((bf16[4,128,512]{2,1,0:T(8,128)(2,1)}), bf16[4,128,512]{2,1,0:T(8,128)(2,1)S(1)}, u32[]{:S(2)}, u32[]{:S(2)}) %all-to-all-start.1) | async-done | bytes 524320 | tf_op jit(solution)/shard_map/all_to_all | solution.py:33
  178.4 0.4 fusion.26
  178.8 0.4 fusion.50
  179.1 0.4 fusion.51
  179.5 0.4 fusion.52
  179.9 0.4 fusion.23
  180.3 0.0 copy-start.3
  180.3 0.8 broadcast_in_dim.98
  181.2 3.7 %all-to-all-start.2 = ((bf16[4,128,512]{2,1,0:T(8,128)(2,1)}), bf16[4,128,512]{2,1,0:T(8,128)(2,1)S(1)}, u32[]{:S(2)}, u32[]{:S(2)}) async-start(bf16[4,128,512]{2,1,0:T(8,128)(2,1)} %broadcast_in_dim.98), calls=%async_computation.2 | async-start | bytes 1048576 | tf_op jit(solution)/shard_map/all_to_all | solution.py:33
  184.8 0.1 select_reduce_fusion
  184.9 8.5 %all-to-all-done.2 = bf16[4,128,512]{2,1,0:T(8,128)(2,1)S(1)} async-done(((bf16[4,128,512]{2,1,0:T(8,128)(2,1)}), bf16[4,128,512]{2,1,0:T(8,128)(2,1)S(1)}, u32[]{:S(2)}, u32[]{:S(2)}) %all-to-all-start.2) | async-done | bytes 524320 | tf_op jit(solution)/shard_map/all_to_all | solution.py:33
  193.4 0.1 multiply_convert_fusion
  193.5 65.0 %all-gather.5.cloned.1.call-done = bf16[4,512,512]{2,1,0:T(8,128)(2,1)} async-done(((bf16[4,8,512]{2,1,0:T(8,128)(2,1)}), bf16[4,512,512]{2,1,0:T(8,128)(2,1)}) %all-gather.5.cloned.1.call-update) | async-done | bytes 2097168 | tf_op jit(solution)/shard_map/all_gather | solution.py:99
  258.5 3.6 %gather_fusion.1 = bf16[64,4,8,512]{3,2,1,0:T(8,128)(2,1)} fusion(bf16[4,64,8,512]{3,2,1,0:T(8,128)(2,1)} %bitcast.79, s32[1024]{0:T(1024)S(1)} %pad_clamp_fusion), kind=kCustom, calls=%fused_computation.1 | custom fusion | bytes 4194560 | tf_op jit(solution)/shard_map/gather | solution.py:104
  262.1 5.5 %fusion.9 = bf16[512,4,512]{0,2,1:T(8,128)(2,1)} fusion(bf16[512,512,1]{1,0,2:T(8,128)(2,1)S(1)} %bitcast.82, f32[4]{0:T(128)S(1)} %get-tuple-element.17, bf16[64,4,8,512]{3,2,1,0:T(8,128)(2,1)S(1)} %bitcast.78, bf16[64,4,8,512]{3,2,1,0:T(8,128)(2,1)} %gather_fusion.1), kind=kOutput, calls=%fused_computation.15 | convolution fusion | flops 2152726528 | bytes 6815760 | tf_op jit(solution)/shard_map/dot_general | solution.py:112
  267.6 3.9 %copy.29 = bf16[512,2048]{1,0:T(8,128)(2,1)} copy(bf16[512,2048]{0,1:T(8,128)(2,1)} %bitcast.80) | data formatting | bytes 4194304
  (19 shorter events, 0.1 us)
Async XLA Ops:
  7.2 3.6 %copy-start.5 = (s32[64]{0:T(128)S(1)}, s32[64]{0:T(128)}, u32[]{:S(2)}) copy-start(s32[64]{0:T(128)} %param.11) | copy-start | bytes 772
  12.8 95.9 %all-to-all-start.3 = ((bf16[64,4,8,512]{3,2,1,0:T(8,128)(2,1)}), bf16[64,4,8,512]{3,2,1,0:T(8,128)(2,1)S(1)}, u32[]{:S(2)}, u32[]{:S(2)}) async-start(bf16[64,4,8,512]{3,2,1,0:T(8,128)(2,1)} %gather_fusion), calls=%async_computation.3 | async-start | bytes 4194304 | tf_op jit(solution)/shard_map/all_to_all | solution.py:27
  27.4 81.2 %copy-start.4 = (s32[4]{0:T(128)S(1)}, s32[4]{0:T(128)}, u32[]{:S(2)}) copy-start(s32[4]{0:T(128)} %param.10) | copy-start | bytes 52
  27.4 118.1 %all-gather.3.cloned.1.call-start = ((), (), s32[]{:S(2)}) async-start(), calls=%async_computation.4 | async-start | bytes 2129920 | tf_op jit(solution)/shard_map/all_gather | solution.py:91
  28.2 230.3 %all-gather.5.cloned.1.call-start = ((), (), s32[]{:S(2)}) async-start(), calls=%async_computation.5 | async-start | bytes 2129920 | tf_op jit(solution)/shard_map/all_gather | solution.py:99
  145.6 2.7 copy-start
  150.1 2.5 copy-start.1
  152.7 12.6 %copy-start.2 = (bf16[1,128,512]{2,1,0:T(8,128)(2,1)S(1)}, bf16[1,128,512]{2,1,0:T(8,128)(2,1)}, u32[]{:S(2)}) copy-start(bf16[1,128,512]{2,1,0:T(8,128)(2,1)} %param.7) | copy-start | bytes 393220
  166.1 12.3 %all-to-all-start.1 = ((bf16[4,128,512]{2,1,0:T(8,128)(2,1)}), bf16[4,128,512]{2,1,0:T(8,128)(2,1)S(1)}, u32[]{:S(2)}, u32[]{:S(2)}) async-start(bf16[4,128,512]{2,1,0:T(8,128)(2,1)} %broadcast_in_dim.97), calls=%async_computation.1 | async-start | bytes 1048576 | tf_op jit(solution)/shard_map/all_to_all | solution.py:33
  180.3 81.8 %copy-start.3 = (bf16[128,512]{1,0:T(8,128)(2,1)}, bf16[128,512]{1,0:T(8,128)(2,1)S(1)}, u32[]{:S(2)}) copy-start(bf16[128,512]{1,0:T(8,128)(2,1)S(1)} %fusion.23) | copy-start | bytes 393220
  181.2 12.3 %all-to-all-start.2 = ((bf16[4,128,512]{2,1,0:T(8,128)(2,1)}), bf16[4,128,512]{2,1,0:T(8,128)(2,1)S(1)}, u32[]{:S(2)}, u32[]{:S(2)}) async-start(bf16[4,128,512]{2,1,0:T(8,128)(2,1)} %broadcast_in_dim.98), calls=%async_computation.2 | async-start | bytes 1048576 | tf_op jit(solution)/shard_map/all_to_all | solution.py:33
Sparse Core Ops, SparseCore 0:
  31.7 113.8 all-gather.2
  152.8 105.6 all-gather.4
where the time goes:
time: 279 us; the launch traced here: 278 us
  waiting for transfers between devices  118 us (42%)
  blocking collectives  87.5 us (31%)
  starting transfers between devices  21.8 us (8%)
  matrix products  19.2 us (7%)
  between operations  16.3 us (6%)
  local copies, waits for them, and re-layouts  11.8 us (4%)
  other arithmetic  3.55 us (1%)
    psum x5, blocking collectives, over_axes(): x = lax.psum(x, axis)  76.2 us
    all_gather x1, waiting for transfers between devices, shards(): lax.all_gather(right_code, GROUP, axis=1, tiled=True)  65 us
    all_gather x1, waiting for transfers between devices, shards(): lax.all_gather(prev_right, GROUP, axis=1, tiled=True).astype(jnp.float32)  36.6 us
    all_to_all x2, waiting for transfers between devices, from_everyone(): return lax.all_to_all(copies, axis, split_axis=0, concat_axis=0, tiled=True)  15.8 us
    all_to_all x1, starting transfers between devices, sent_and_summed(): lax.all_to_all(pieces, axis, split_axis=0, concat_axis=0, tiled=True)  14.6 us
    all_to_all x1, blocking collectives, sent_and_summed(): lax.all_to_all(pieces, axis, split_axis=0, concat_axis=0, tiled=True)  11.3 us
    dot_general x10, matrix products, newton_rows(): product = jnp.matmul(product, start_root, precision=lax.Precision.HIGHEST)  8.9 us
    all_to_all x2, starting transfers between devices, from_everyone(): return lax.all_to_all(copies, axis, split_axis=0, concat_axis=0, tiled=True)  7.12 us
  transfers between devices with their start and end apart: 5, of which 4 were waited for; matrix products, arithmetic and copies ran while one was open for 3% of the time, Pallas kernels for 0%

commit v1 on v0

--- a/solution.py
+++ b/solution.py
@@ -96,7 +96,14 @@
     left_code = (left_new * pow_two(-exp_left[0])).astype(jnp.bfloat16)
     right_code = (right_new * pow_two(-exp_right)[:, None, None]).astype(jnp.bfloat16)
     left_full = collect(left_code, REPLICA, 0)
-    right_owned = lax.all_gather(right_code, GROUP, axis=1, tiled=True).reshape(
+
+    def levels_all_tell(view, chip_axis):
+        far_arr = jnp.concatenate(
+            lax.all_to_all(jnp.stack(lax.axis_size(chip_axis) * [view]), chip_axis, 0, 0), axis=1
+        )
+        return far_arr
+
+    right_owned = levels_all_tell(right_code, GROUP).reshape(
         col_count, groups, strip_rows, block_size
     )
     owner_match = strip_owner[:, None] == jnp.arange(groups)[None, :]

time: 279 us -> 256 us (0.918)
  waiting for transfers between devices: 118 us -> 87.6 us
  blocking collectives: 87.5 us -> 75.3 us
  starting transfers between devices: 21.8 us -> 32.9 us
  local copies, waits for them, and re-layouts: 11.8 us -> 17.6 us
    all_gather x1 -> x0, waiting for transfers between devices: 65 us -> none  [shards(): lax.all_gather(right_code, GROUP, axis=1, tiled=True)]
    all_to_all x0 -> x1, waiting for transfers between devices: none -> 46.7 us  [levels_all_tell(): lax.all_to_all(jnp.stack(lax.axis_size(chip_axis) * [view]), chip_axis, 0...]
    all_to_all x2, waiting for transfers between devices: 15.8 us -> 3.68 us  [from_everyone(): return lax.all_to_all(copies, axis, split_axis=0, concat_axis=0, tiled=True)]
    all_to_all x1 -> x0, blocking collectives: 11.3 us -> none  [sent_and_summed(): lax.all_to_all(pieces, axis, split_axis=0, concat_axis=0, tiled=True)]
    all_to_all x0 -> x1, starting transfers between devices: none -> 7.81 us  [levels_all_tell(): lax.all_to_all(jnp.stack(lax.axis_size(chip_axis) * [view]), chip_axis, 0...]
    all_to_all x1 -> x2, starting transfers between devices: 14.6 us -> 18.1 us  [sent_and_summed(): lax.all_to_all(pieces, axis, split_axis=0, concat_axis=0, tiled=True)]
    dot_general x1, matrix products: 1.28 us -> 4.45 us  [shards(): lax.dot_general(grad, grad, (((1,), (1,)), ((), ())), preferred_element_t...]
  transfers between devices with their start and end apart: 5 -> 6, of which waited for: 4 -> 4; matrix products, arithmetic and copies ran while one was open for 3% -> 10% of each run, Pallas kernels for 0% -> 0%
where the time goes in v1:
time: 256 us; the launch traced here: 255 us
  waiting for transfers between devices  87.6 us (34%)
  blocking collectives  75.3 us (29%)
  starting transfers between devices  32.9 us (13%)
  matrix products  20.8 us (8%)
  local copies, waits for them, and re-layouts  17.6 us (7%)
  between operations  16.3 us (6%)
  other arithmetic  4.21 us (2%)
    psum x5, blocking collectives, over_axes(): x = lax.psum(x, axis)  75.3 us
    all_to_all x1, waiting for transfers between devices, levels_all_tell(): lax.all_to_all(jnp.stack(lax.axis_size(chip_axis) * [view]), chip_axis, 0...  46.7 us
    all_gather x1, waiting for transfers between devices, shards(): lax.all_gather(prev_right, GROUP, axis=1, tiled=True).astype(jnp.float32)  34 us
    all_to_all x2, starting transfers between devices, sent_and_summed(): lax.all_to_all(pieces, axis, split_axis=0, concat_axis=0, tiled=True)  18.1 us
    dot_general x10, matrix products, newton_rows(): product = jnp.matmul(product, start_root, precision=lax.Precision.HIGHEST)  8.3 us
    all_to_all x1, starting transfers between devices, levels_all_tell(): lax.all_to_all(jnp.stack(lax.axis_size(chip_axis) * [view]), chip_axis, 0...  7.81 us
    all_to_all x2, starting transfers between devices, from_everyone(): return lax.all_to_all(copies, axis, split_axis=0, concat_axis=0, tiled=True)  6.94 us
    dot_general x1, matrix products, shards(): lax.dot_general(left_dec, middle, (((1,), (1,)), ((), ())), preferred_ele...  5.44 us
  transfers between devices with their start and end apart: 6, of which 4 were waited for; matrix products, arithmetic and copies ran while one was open for 10% of the time, Pallas kernels for 0%

profile of v1, /device:TPU:2, one launch (start us, length us, event | category | flops | bytes accessed | tf_op | source)
XLA Modules:
  0.0 254.7 jit_solution(10504611951206013926)
XLA Ops:
  7.2 1.7 broadcast_in_dim.97
  8.9 3.5 %all-to-all-start.1 = ((bf16[4,128,512]{2,1,0:T(8,128)(2,1)}), bf16[4,128,512]{2,1,0:T(8,128)(2,1)S(1)}, u32[]{:S(2)}, u32[]{:S(2)}) async-start(bf16[4,128,512]{2,1,0:T(8,128)(2,1)} %broadcast_in_dim.97), calls=%async_computation.1 | async-start | bytes 1048576 | tf_op jit(solution)/shard_map/all_to_all | solution.py:33
  12.4 0.7 compare_select_fusion.1
  13.0 4.5 %convolution_convert_fusion = bf16[512,512]{1,0:T(8,128)(2,1)} fusion(bf16[512,2048]{1,0:T(8,128)(2,1)} %param.6), kind=kOutput, calls=%fused_computation.19 | convolution fusion | flops 1074003968 | bytes 2621440 | tf_op jit(solution)/shard_map/dot_general | solution.py:79
  17.5 3.7 %all-to-all-done.1 = bf16[4,128,512]{2,1,0:T(8,128)(2,1)S(1)} async-done(((bf16[4,128,512]{2,1,0:T(8,128)(2,1)}), bf16[4,128,512]{2,1,0:T(8,128)(2,1)S(1)}, u32[]{:S(2)}, u32[]{:S(2)}) %all-to-all-start.1) | async-done | bytes 524320 | tf_op jit(solution)/shard_map/all_to_all | solution.py:33
  21.2 3.5 %all-to-all-start = ((bf16[4,128,512]{2,1,0:T(8,128)(2,1)}), bf16[4,128,512]{2,1,0:T(8,128)(2,1)S(1)}, u32[]{:S(2)}, u32[]{:S(2)}) async-start(bf16[4,128,512]{2,1,0:T(8,128)(2,1)} %bitcast.83), calls=%async_computation | async-start | bytes 1048576 | tf_op jit(solution)/shard_map/all_to_all | solution.py:27
  24.7 2.6 %convolution_bitcast_fusion = bf16[4,64,8,512]{3,2,1,0:T(8,128)(2,1)} fusion(bf16[64,4,8,512]{3,2,1,0:T(8,128)(2,1)S(1)} %bitcast.80), kind=kOutput, calls=%fused_computation.7 | convolution fusion | flops 1073741824 | bytes 4194304 | tf_op jit(solution)/shard_map/dot_general | solution.py:82
  27.3 3.6 %gather_fusion = bf16[64,4,8,512]{3,2,1,0:T(8,128)(2,1)} fusion(bf16[4,64,8,512]{3,2,1,0:T(8,128)(2,1)} %convolution_bitcast_fusion, s32[1024]{0:T(1024)S(1)} %pad_clamp_fusion.1), kind=kCustom, calls=%fused_computation | custom fusion | bytes 4194560 | tf_op jit(solution)/shard_map/gather | solution.py:87
  30.9 2.5 all-to-all-done
  33.4 14.6 %all-to-all-start.3 = ((bf16[64,4,8,512]{3,2,1,0:T(8,128)(2,1)}), bf16[64,4,8,512]{3,2,1,0:T(8,128)(2,1)S(1)}, u32[]{:S(2)}, u32[]{:S(2)}) async-start(bf16[64,4,8,512]{3,2,1,0:T(8,128)(2,1)} %gather_fusion), calls=%async_computation.3 | async-start | bytes 4194304 | tf_op jit(solution)/shard_map/all_to_all | solution.py:27
  48.1 0.0 all-gather.2.cloned.1.call-start
  48.1 0.7 all-gather.2.cloned.1.call-update
  48.8 0.6 dynamic_slice.6
  50.1 2.0 multiply_reduce_fusion
  52.8 0.1 reduce_sum.66
  53.0 0.1 broadcast_multiply_fusion.1
  53.1 0.1 broadcast_multiply_fusion
  53.1 52.6 %psum.35 = f32[64,4,4]{0,2,1:T(4,128)S(1)} all-reduce(f32[64,4,4]{0,2,1:T(4,128)S(1)} %broadcast_multiply_fusion), channel_id=1, replica_groups=mesh['group_0'=8,'group_1'=2,'group_2'=4,'replica_0'=2,'replica_1'=2] {'..., use_global_device_ids=true, to_apply=%region_3.0 | all-reduce | flops 1024 | bytes 8192 | tf_op jit(solution)/shard_map/psum | solution.py:15
  105.7 6.5 %psum.36 = f32[64,4,4]{0,2,1:T(4,128)S(1)} all-reduce(f32[64,4,4]{0,2,1:T(4,128)S(1)} %psum.35), channel_id=1, replica_groups=mesh['group_0'=8,'group_1'=2,'group_2'=4,'replica_0'=2,'replica_1'=2] {'..., use_global_device_ids=true, to_apply=%region_4.0 | all-reduce | flops 1024 | bytes 8192 | tf_op jit(solution)/shard_map/psum | solution.py:15
  112.2 8.7 %psum.37 = f32[64,4,4]{0,2,1:T(4,128)S(1)} all-reduce(f32[64,4,4]{0,2,1:T(4,128)S(1)} %psum.36), channel_id=1, replica_groups=mesh['group_0'=8,'group_1'=2,'group_2'=4,'replica_0'=2,'replica_1'=2] {'..., use_global_device_ids=true, to_apply=%region_5.0 | all-reduce | flops 1024 | bytes 8192 | tf_op jit(solution)/shard_map/psum | solution.py:15
  121.0 5.0 %psum.38 = f32[64,4,4]{0,2,1:T(4,128)S(1)} all-reduce(f32[64,4,4]{0,2,1:T(4,128)S(1)} %psum.37), channel_id=1, replica_groups=mesh['group_0'=8,'group_1'=2,'group_2'=4,'replica_0'=2,'replica_1'=2] {'..., use_global_device_ids=true, to_apply=%region_6.0 | all-reduce | flops 1024 | bytes 8192 | tf_op jit(solution)/shard_map/psum | solution.py:15
  126.0 2.5 psum.39
  128.4 0.6 multiply_reduce_fusion.1
  129.7 0.1 convert_reduce_fusion.1
  129.8 0.4 fusion.26
  130.2 0.4 fusion.50
  130.6 0.4 fusion.51
  131.0 0.4 fusion.52
  131.4 0.4 fusion.23
  131.8 0.8 broadcast_in_dim.98
  132.6 3.5 %all-to-all-start.2 = ((bf16[4,128,512]{2,1,0:T(8,128)(2,1)}), bf16[4,128,512]{2,1,0:T(8,128)(2,1)S(1)}, u32[]{:S(2)}, u32[]{:S(2)}) async-start(bf16[4,128,512]{2,1,0:T(8,128)(2,1)} %broadcast_in_dim.98), calls=%async_computation.2 | async-start | bytes 1048576 | tf_op jit(solution)/shard_map/all_to_all | solution.py:33
  136.1 0.3 convert_reduce_fusion
  136.4 34.0 %all-gather.2.cloned.1.call-done = bf16[4,512,512]{2,1,0:T(8,128)(2,1)} async-done(((bf16[4,8,512]{2,1,0:T(8,128)(2,1)}), bf16[4,512,512]{2,1,0:T(8,128)(2,1)}) %all-gather.2.cloned.1.call-update) | async-done | bytes 2097168 | tf_op jit(solution)/shard_map/all_gather | solution.py:91
  170.5 2.7 %fusion.29 = f32[4,8,512]{2,1,0:T(8,128)S(1)} fusion(bf16[4,512,512]{2,1,0:T(8,128)(2,1)} %all-gather.2.cloned.1.call-done, f32[4,8,512]{2,1,0:T(8,128)S(1)} %convert_reduce_fusion, f32[4]{0:T(128)S(1)} %multiply_add_fusion), kind=kOutput, calls=%fused_computation.31 | convolution fusion | flops 100679680 | bytes 2228240 | tf_op jit(solution)/shard_map/dot_general | solution.py:57
  173.2 0.9 fusion.53
  174.1 0.9 fusion.54
  175.0 0.9 fusion.55
  176.0 0.9 fusion.25
  176.9 0.0 all-to-all-done.2
  176.9 1.6 stack.2
  178.5 7.8 %all-to-all-start.4 = ((bf16[64,4,8,512]{3,2,1,0:T(8,128)(2,1)}), bf16[64,4,8,512]{3,2,1,0:T(8,128)(2,1)S(1)}, u32[]{:S(2)}, u32[]{:S(2)}) async-start(bf16[64,4,8,512]{3,2,1,0:T(8,128)(2,1)} %stack.2), calls=%async_computation.4 | async-start | bytes 4194304 | tf_op jit(solution)/shard_map/all_to_all | solution.py:102
  186.4 0.1 select_reduce_fusion
  186.5 0.1 multiply_convert_fusion
  186.6 46.7 %all-to-all-done.4 = bf16[64,4,8,512]{3,2,1,0:T(8,128)(2,1)S(1)} async-done(((bf16[64,4,8,512]{3,2,1,0:T(8,128)(2,1)}), bf16[64,4,8,512]{3,2,1,0:T(8,128)(2,1)S(1)}, u32[]{:S(2)}, u32[]{:S(2)}) %all-to-all-start.4) | async-done | bytes 2097184 | tf_op jit(solution)/shard_map/all_to_all | solution.py:102
  233.2 1.5 copy.61
  234.8 3.8 %gather_fusion.1 = bf16[64,4,8,512]{3,2,1,0:T(8,128)(2,1)} fusion(bf16[4,64,8,512]{3,2,1,0:T(8,128)(2,1)} %bitcast.79, s32[1024]{0:T(1024)S(1)} %pad_clamp_fusion), kind=kCustom, calls=%fused_computation.1 | custom fusion | bytes 4194560 | tf_op jit(solution)/shard_map/gather | solution.py:111
  238.5 5.4 %fusion.9 = bf16[512,4,512]{0,2,1:T(8,128)(2,1)} fusion(bf16[512,512,1]{1,0,2:T(8,128)(2,1)S(1)} %bitcast.84, f32[4]{0:T(128)S(1)} %get-tuple-element.20, bf16[64,4,8,512]{3,2,1,0:T(8,128)(2,1)S(1)} %bitcast.81, bf16[64,4,8,512]{3,2,1,0:T(8,128)(2,1)} %gather_fusion.1), kind=kOutput, calls=%fused_computation.16 | convolution fusion | flops 2152726528 | bytes 6815760 | tf_op jit(solution)/shard_map/dot_general | solution.py:119
  244.0 3.9 %copy.38 = bf16[512,2048]{1,0:T(8,128)(2,1)} copy(bf16[512,2048]{0,1:T(8,128)(2,1)} %bitcast.82) | data formatting | bytes 4194304
  (25 shorter events, 0.1 us)
Async XLA Ops:
  8.9 12.3 %all-to-all-start.1 = ((bf16[4,128,512]{2,1,0:T(8,128)(2,1)}), bf16[4,128,512]{2,1,0:T(8,128)(2,1)S(1)}, u32[]{:S(2)}, u32[]{:S(2)}) async-start(bf16[4,128,512]{2,1,0:T(8,128)(2,1)} %broadcast_in_dim.97), calls=%async_computation.1 | async-start | bytes 1048576 | tf_op jit(solution)/shard_map/all_to_all | solution.py:33
  13.0 11.6 %copy-start.1 = (bf16[512,2048]{1,0:T(8,128)(2,1)S(1)}, bf16[512,2048]{1,0:T(8,128)(2,1)}, u32[]{:S(2)}) copy-start(bf16[512,2048]{1,0:T(8,128)(2,1)} %param.6) | copy-start | bytes 6291460
  21.2 12.3 %all-to-all-start = ((bf16[4,128,512]{2,1,0:T(8,128)(2,1)}), bf16[4,128,512]{2,1,0:T(8,128)(2,1)S(1)}, u32[]{:S(2)}, u32[]{:S(2)}) async-start(bf16[4,128,512]{2,1,0:T(8,128)(2,1)} %bitcast.83), calls=%async_computation | async-start | bytes 1048576 | tf_op jit(solution)/shard_map/all_to_all | solution.py:27
  30.9 17.9 %copy-start.7 = (s32[64]{0:T(128)S(1)}, s32[64]{0:T(128)}, u32[]{:S(2)}) copy-start(s32[64]{0:T(128)} %param.11) | copy-start | bytes 772
  33.4 98.4 %all-to-all-start.3 = ((bf16[64,4,8,512]{3,2,1,0:T(8,128)(2,1)}), bf16[64,4,8,512]{3,2,1,0:T(8,128)(2,1)S(1)}, u32[]{:S(2)}, u32[]{:S(2)}) async-start(bf16[64,4,8,512]{3,2,1,0:T(8,128)(2,1)} %gather_fusion), calls=%async_computation.3 | async-start | bytes 4194304 | tf_op jit(solution)/shard_map/all_to_all | solution.py:27
  48.1 81.6 %copy-start.6 = (s32[4]{0:T(128)S(1)}, s32[4]{0:T(128)}, u32[]{:S(2)}) copy-start(s32[4]{0:T(128)} %param.10) | copy-start | bytes 52
  48.1 122.4 %all-gather.2.cloned.1.call-start = ((), (), s32[]{:S(2)}) async-start(), calls=%async_computation.5 | async-start | bytes 2129920 | tf_op jit(solution)/shard_map/all_gather | solution.py:91
  129.8 1.6 copy-start.3
  131.8 41.4 %copy-start.4 = (bf16[128,512]{1,0:T(8,128)(2,1)}, bf16[128,512]{1,0:T(8,128)(2,1)S(1)}, u32[]{:S(2)}) copy-start(bf16[128,512]{1,0:T(8,128)(2,1)S(1)} %fusion.23) | copy-start | bytes 393220
  132.6 44.3 %all-to-all-start.2 = ((bf16[4,128,512]{2,1,0:T(8,128)(2,1)}), bf16[4,128,512]{2,1,0:T(8,128)(2,1)S(1)}, u32[]{:S(2)}, u32[]{:S(2)}) async-start(bf16[4,128,512]{2,1,0:T(8,128)(2,1)} %broadcast_in_dim.98), calls=%async_computation.2 | async-start | bytes 1048576 | tf_op jit(solution)/shard_map/all_to_all | solution.py:33
  170.5 2.7 %copy-start = (bf16[4,512,512]{2,1,0:T(8,128)(2,1)S(1)}, bf16[4,512,512]{2,1,0:T(8,128)(2,1)}, u32[]{:S(2)}) copy-start(bf16[4,512,512]{2,1,0:T(8,128)(2,1)} %all-gather.2.cloned.1.call-done) | copy-start | bytes 6291460
  176.9 1.6 copy-start.5
  178.5 54.7 %all-to-all-start.4 = ((bf16[64,4,8,512]{3,2,1,0:T(8,128)(2,1)}), bf16[64,4,8,512]{3,2,1,0:T(8,128)(2,1)S(1)}, u32[]{:S(2)}, u32[]{:S(2)}) async-start(bf16[64,4,8,512]{3,2,1,0:T(8,128)(2,1)} %stack.2), calls=%async_computation.4 | async-start | bytes 4194304 | tf_op jit(solution)/shard_map/all_to_all | solution.py:102
  234.8 3.8 %copy-start.2 = (bf16[512,2048]{1,0:T(8,128)(2,1)S(1)}, bf16[512,2048]{1,0:T(8,128)(2,1)}, u32[]{:S(2)}) copy-start(bf16[512,2048]{1,0:T(8,128)(2,1)} %param.6) | copy-start | bytes 6291460
Sparse Core Ops, SparseCore 0:
  52.4 118.0 all-gather.1
